TPU v7x, 32 devices: a whole 2x2x4 slice. The times are simulated.
32 devices in a mesh: rows: 8 (over z, x), head: 4 (over y, core).
Axes of the slice: x: 2, y: 2, z: 4, core: 2. Of those that a mesh axis runs over, the one named last changes fastest.
Arguments:
- inputs: bfloat16 [2, 32, 512, 768], P(None, ('rows', 'head')), may hold values from -6 to 6
- qkv_weight: bfloat16 [768, 2304], P('rows', 'head'), may hold values from -0.3125 to 0.3125
- out_weight: bfloat16 [768, 768], P('rows', 'head'), may hold values from -0.625 to 0.625
- up_weight: bfloat16 [768, 3072], P('rows', 'head'), may hold values from -0.21875 to 0.21875
- down_weight: bfloat16 [3072, 768], P('rows', 'head'), may hold values from -0.109375 to 0.109375
- biases: bfloat16 [8, 768], P('head', 'rows'), may hold values from -1.1953125 to 1.1953125
- norm_params: bfloat16 [4, 768], P('head', 'rows'), may hold values from -0.6 to 1.65
- cotangent: bfloat16 [2, 32, 512, 768], P(None, ('rows', 'head')), may hold values from -6 to 6
- boundaries: int32 [2, 32], P(None, 'rows'), may hold values from 1 to 511, as said below
- lengths: int32 [2, 32], P(None, 'rows'), may hold values from 257 to 512, as said below
Outputs:
- output: bfloat16 [2, 32, 512, 768], P(None, ('rows', 'head'))
- input_grad: float32 [2, 32, 512, 768], P(None, ('rows', 'head'))
- qkv_grad: float32 [768, 2304], P('rows', 'head')
- out_grad: float32 [768, 768], P('rows', 'head')
- up_grad: float32 [768, 3072], P('rows', 'head')
- down_grad: float32 [3072, 768], P('rows', 'head')
- bias_grad: float32 [8, 768], P('head', 'rows')
- norm_grad: float32 [4, 768], P('head', 'rows')
Inputs may be any that keep to these rules, and one draw needn't show every extreme that they name: `boundaries`: each row's boundary lies below its own length, so both sentences of a row hold tokens. `lengths`: every length exceeds half of 512.
All inputs are finite; a program needn't handle non-finite values.
Results may differ from a plain program's by a relative error of at most 0.017.
The roundings to bfloat16 on the way count: a program that leaves them out, or rounds other values in their place, can miss the bound.
Values may be sent and summed in bfloat16 or wider, within the bound.
A program may use at most 192 MiB of HBM per device.

v0:
```python
import jax
import jax.numpy as jnp
from jax import lax
from jax.sharding import PartitionSpec as P

D = 768
HEADS = 12
HD = 64
FF = 3072
SEQ = 512
EPSILON = 1e-06
ROOT_HALF = 0.7071067811865476
INVERSE_ROOT_TWO_PI = 0.3989422804014327


def contract_rows(left, right):
    return lax.dot_general(
        left, right, (((0,), (0,)), ((), ())), preferred_element_type=jnp.float32
    )


def contract_cols(left, right):
    return lax.dot_general(
        left, right, (((1,), (1,)), ((), ())), preferred_element_type=jnp.float32
    )


def norm_forward(values_in, gain_row, shift_row):
    average = jnp.mean(values_in, axis=-1, keepdims=True)
    centered = values_in - average
    variance = jnp.mean(centered * centered, axis=-1, keepdims=True)
    inverse_scale = lax.rsqrt(variance + EPSILON)
    normed = centered * inverse_scale
    return (normed * gain_row + shift_row, normed, inverse_scale)


def norm_backward(grad_out, normed, inverse_scale, gain_row):
    grad_normed = grad_out * gain_row
    first_mean = jnp.mean(grad_normed, axis=-1, keepdims=True)
    second_mean = jnp.mean(grad_normed * normed, axis=-1, keepdims=True)
    grad_in = inverse_scale * (grad_normed - first_mean - normed * second_mean)
    return (grad_in, jnp.sum(grad_out * normed, axis=0), jnp.sum(grad_out, axis=0))


def masked_scores(queries, keys_in, bound, length):
    positions = lax.broadcasted_iota(jnp.int32, (SEQ,), 0)
    segment = positions >= bound
    allowed = (segment[:, None] == segment[None, :]) & (positions[None, :] < length)
    scores = jnp.einsum(
        "qhe,khe->hqk", queries, keys_in, preferred_element_type=jnp.float32
    ) * HD ** (-0.5)
    return jnp.where(allowed[None], scores, -1e30)


def attend_forward(pieces):
    queries, keys_in, values_in, bound, length = pieces
    scores = masked_scores(queries, keys_in, bound, length)
    highest = jnp.max(scores, axis=-1, keepdims=True)
    raised = jnp.exp(scores - highest)
    totals = jnp.sum(raised, axis=-1, keepdims=True)
    weights_low = (raised / totals).astype(jnp.bfloat16)
    context = jnp.einsum("hqk,khe->qhe", weights_low, values_in, preferred_element_type=jnp.float32)
    log_total = (highest + jnp.log(totals))[..., 0]
    return (context.astype(jnp.bfloat16), log_total)


def attend_backward(pieces):
    queries, keys_in, values_in, bound, length, log_total, grad_context = pieces
    scores = masked_scores(queries, keys_in, bound, length)
    weights_full = jnp.exp(scores - log_total[..., None])
    weights_low = weights_full.astype(jnp.bfloat16)
    grad_values = jnp.einsum(
        "hqk,qhe->khe", weights_low, grad_context, preferred_element_type=jnp.float32
    )
    grad_weights = jnp.einsum(
        "qhe,khe->hqk", grad_context, values_in, preferred_element_type=jnp.float32
    )
    inner_sum = jnp.sum(weights_full * grad_weights, axis=-1, keepdims=True)
    grad_scores = (weights_full * (grad_weights - inner_sum)).astype(jnp.bfloat16)
    grad_queries = jnp.einsum(
        "hqk,khe->qhe", grad_scores, keys_in, preferred_element_type=jnp.float32
    ) * HD ** (-0.5)
    grad_keys = jnp.einsum(
        "hqk,qhe->khe", grad_scores, queries, preferred_element_type=jnp.float32
    ) * HD ** (-0.5)
    return jnp.stack([grad_queries, grad_keys, grad_values], axis=2).astype(jnp.bfloat16)


def split_heads(project, bounds, lengths_here, groups):
    seq_per = project.shape[0] // SEQ
    heads_dev = HEADS // groups
    spread = project.reshape(seq_per, SEQ, groups, 3 * D // groups)
    items = lax.all_to_all(spread, "head", split_axis=2, concat_axis=0, tiled=True)
    return (items.reshape(-1, SEQ, heads_dev, 3, HD), bounds, lengths_here)


def merge_heads(context_items, seq_per):
    width = context_items.shape[2] * HD
    joined = lax.all_to_all(
        context_items.reshape(-1, SEQ, 1, width), "head", split_axis=0, concat_axis=2, tiled=True
    )
    return joined.reshape(seq_per * SEQ, D)


def grad_to_items(grad_context, seq_per, groups):
    heads_dev = HEADS // groups
    spread = grad_context.reshape(seq_per, SEQ, groups, D // groups)
    items = lax.all_to_all(spread, "head", split_axis=2, concat_axis=0, tiled=True)
    return items.reshape(-1, SEQ, heads_dev, HD)


def grad_to_tokens(grad_items, seq_per):
    width = grad_items.shape[2] * 3 * HD
    joined = lax.all_to_all(
        grad_items.reshape(-1, SEQ, 1, width), "head", split_axis=0, concat_axis=2, tiled=True
    )
    return joined.reshape(seq_per * SEQ, 3 * D)


def gather_weights(qkv_weight, out_weight, up_weight, down_weight, biases, norm_params):
    by_head = (
        lax.all_gather(qkv_weight, "head", axis=1, tiled=True),
        lax.all_gather(out_weight, "head", axis=1, tiled=True),
        lax.all_gather(up_weight, "head", axis=1, tiled=True),
        lax.all_gather(down_weight, "head", axis=1, tiled=True),
        lax.all_gather(biases, "head", axis=0, tiled=True),
        lax.all_gather(norm_params, "head", axis=0, tiled=True),
    )
    return (
        lax.all_gather(by_head[0], "rows", axis=0, tiled=True),
        lax.all_gather(by_head[1], "rows", axis=0, tiled=True),
        lax.all_gather(by_head[2], "rows", axis=0, tiled=True),
        lax.all_gather(by_head[3], "rows", axis=0, tiled=True),
        lax.all_gather(by_head[4], "rows", axis=1, tiled=True),
        lax.all_gather(by_head[5], "rows", axis=1, tiled=True),
    )


def reduce_grads(running):
    rows_done = (
        lax.psum_scatter(running[0], "rows", scatter_dimension=0, tiled=True),
        lax.psum_scatter(running[1], "rows", scatter_dimension=0, tiled=True),
        lax.psum_scatter(running[2], "rows", scatter_dimension=0, tiled=True),
        lax.psum_scatter(running[3], "rows", scatter_dimension=0, tiled=True),
        lax.psum_scatter(running[4], "rows", scatter_dimension=1, tiled=True),
        lax.psum_scatter(running[5], "rows", scatter_dimension=1, tiled=True),
    )
    return (
        lax.psum_scatter(
            rows_done[0].astype(jnp.bfloat16), "head", scatter_dimension=1, tiled=True
        ).astype(jnp.float32),
        lax.psum_scatter(
            rows_done[1].astype(jnp.bfloat16), "head", scatter_dimension=1, tiled=True
        ).astype(jnp.float32),
        lax.psum_scatter(
            rows_done[2].astype(jnp.bfloat16), "head", scatter_dimension=1, tiled=True
        ).astype(jnp.float32),
        lax.psum_scatter(
            rows_done[3].astype(jnp.bfloat16), "head", scatter_dimension=1, tiled=True
        ).astype(jnp.float32),
        lax.psum_scatter(
            rows_done[4].astype(jnp.bfloat16), "head", scatter_dimension=0, tiled=True
        ).astype(jnp.float32),
        lax.psum_scatter(
            rows_done[5].astype(jnp.bfloat16), "head", scatter_dimension=0, tiled=True
        ).astype(jnp.float32),
    )


def layer_step(params, block_in, block_cot, bounds, lengths_here):
    qkv_full, out_full, up_full, down_full, bias_full, norm_full = params
    seq_per = block_in.shape[0]
    groups = lax.axis_size("head")
    tokens = block_in.reshape(seq_per * SEQ, D)
    bias_float = bias_full.astype(jnp.float32)
    norm_float = norm_full.astype(jnp.float32)
    zero_part = jnp.zeros((HEADS, HD), jnp.float32)
    head_bias = jnp.stack(
        [bias_float[0].reshape(HEADS, HD), zero_part, bias_float[1].reshape(HEADS, HD)], axis=1
    ).reshape(3 * D)
    project = (jnp.dot(tokens, qkv_full, preferred_element_type=jnp.float32) + head_bias).astype(
        jnp.bfloat16
    )
    items, item_bounds, item_lengths = split_heads(project, bounds, lengths_here, groups)
    queries = items[:, :, :, 0]
    keys_all = items[:, :, :, 1]
    values_all = items[:, :, :, 2]
    context_items, log_total = lax.map(
        attend_forward, (queries, keys_all, values_all, item_bounds, item_lengths)
    )
    context_tok = merge_heads(context_items, seq_per)
    attended = jnp.dot(context_tok, out_full, preferred_element_type=jnp.float32) + bias_float[2]
    hidden, normed_one, scale_one = norm_forward(
        tokens.astype(jnp.float32) + attended, norm_float[0], norm_float[1]
    )
    hidden_low = hidden.astype(jnp.bfloat16)
    inner_pre = jnp.dot(hidden_low, up_full, preferred_element_type=jnp.float32) + bias_float[
        4:8
    ].reshape(FF)
    active_low = jax.nn.gelu(inner_pre, approximate=False).astype(jnp.bfloat16)
    outer_out = jnp.dot(active_low, down_full, preferred_element_type=jnp.float32) + bias_float[3]
    output_float, normed_two, scale_two = norm_forward(
        hidden + outer_out, norm_float[2], norm_float[3]
    )
    output_block = output_float.astype(jnp.bfloat16).reshape(seq_per, SEQ, D)
    grad_out = block_cot.reshape(seq_per * SEQ, D).astype(jnp.float32)
    grad_two, gain_two, shift_two = norm_backward(grad_out, normed_two, scale_two, norm_float[2])
    grad_two_low = grad_two.astype(jnp.bfloat16)
    down_grad = contract_rows(active_low, grad_two_low)
    grad_active = contract_cols(grad_two_low, down_full)
    slope = (
        0.5 * (1.0 + lax.erf(inner_pre * ROOT_HALF))
        + inner_pre * jnp.exp(-0.5 * inner_pre * inner_pre) * INVERSE_ROOT_TWO_PI
    )
    grad_inner = grad_active * slope
    grad_inner_low = grad_inner.astype(jnp.bfloat16)
    up_grad = contract_rows(hidden_low, grad_inner_low)
    grad_hidden = contract_cols(grad_inner_low, up_full) + grad_two
    grad_one, gain_one, shift_one = norm_backward(grad_hidden, normed_one, scale_one, norm_float[0])
    grad_one_low = grad_one.astype(jnp.bfloat16)
    out_grad = contract_rows(context_tok, grad_one_low)
    grad_context = contract_cols(grad_one_low, out_full).astype(jnp.bfloat16)
    grad_items = grad_to_items(grad_context, seq_per, groups)
    grad_project_items = lax.map(
        attend_backward,
        (queries, keys_all, values_all, item_bounds, item_lengths, log_total, grad_items),
    )
    grad_project = grad_to_tokens(grad_project_items, seq_per)
    qkv_grad = contract_rows(tokens, grad_project)
    grad_input = contract_cols(grad_project, qkv_full) + grad_one
    project_sums = jnp.sum(grad_project, axis=0, dtype=jnp.float32).reshape(HEADS, 3, HD)
    bias_grad = jnp.concatenate(
        [
            project_sums[:, 0].reshape(1, D),
            project_sums[:, 2].reshape(1, D),
            jnp.sum(grad_one, axis=0).reshape(1, D),
            jnp.sum(grad_two, axis=0).reshape(1, D),
            jnp.sum(grad_inner, axis=0).reshape(4, D),
        ],
        axis=0,
    )
    norm_grad = jnp.stack([gain_one, shift_one, gain_two, shift_two])
    return (
        output_block,
        grad_input.reshape(seq_per, SEQ, D),
        (qkv_grad, out_grad, up_grad, down_grad, bias_grad, norm_grad),
    )


def shards(
    inputs,
    qkv_weight,
    out_weight,
    up_weight,
    down_weight,
    biases,
    norm_params,
    cotangent,
    boundaries,
    lengths,
):
    outputs_all = []
    inputs_grads = []
    running = None
    for micro_index in range(inputs.shape[0]):
        params = gather_weights(qkv_weight, out_weight, up_weight, down_weight, biases, norm_params)
        output_block, grad_block, grads_now = layer_step(
            params,
            inputs[micro_index],
            cotangent[micro_index],
            boundaries[micro_index],
            lengths[micro_index],
        )
        outputs_all.append(output_block)
        inputs_grads.append(grad_block)
        if micro_index == 0:
            running = grads_now
        else:
            running = tuple((sum_now + add_now for sum_now, add_now in zip(running, grads_now)))
    final = reduce_grads(running)
    return (
        jnp.stack(outputs_all),
        jnp.stack(inputs_grads),
        final[0],
        final[1],
        final[2],
        final[3],
        final[4],
        final[5],
    )


def solution(mesh):
    placed = (
        P(None, ("rows", "head"), None, None),
        P("rows", "head"),
        P("rows", "head"),
        P("rows", "head"),
        P("rows", "head"),
        P("head", "rows"),
        P("head", "rows"),
        P(None, ("rows", "head"), None, None),
        P(None, "rows"),
        P(None, "rows"),
    )
    return jax.shard_map(
        shards,
        mesh=mesh,
        in_specs=placed,
        out_specs=(
            P(None, ("rows", "head"), None, None),
            P(None, ("rows", "head"), None, None),
            P("rows", "head"),
            P("rows", "head"),
            P("rows", "head"),
            P("rows", "head"),
            P("head", "rows"),
            P("head", "rows"),
        ),
        check_vma=False,
    )
```

profile of v0, /device:TPU:0, one launch (start us, length us, event | category | flops | bytes accessed | tf_op | source)
XLA Modules:
  0.0 1183.9 jit_solution(4016477285375403573)
XLA Ops:
  7.2 8.8 all-gather
  18.5 5.6 all_gather.52
  25.0 8.1 all_gather.56
  33.1 5.1 all-gather.1
  38.1 27.4 %all-gather.2 = bf16[8,96,8]{1,2,0:T(8,128)(2,1)S(1)} all-gather(bf16[1,96,8]{1,2,0:T(8,128)(2,1)S(1)} %bitcast.451), channel_id=1, replica_groups=mesh['rows'=8,'head'=4] {'rows'}, dimensions={0}, use_global_device_ids=true | all-gather | bytes 13824 | tf_op jit(solution)/shard_map/all_gather | solution.py:134
  66.6 16.7 %all-gather.10.cloned.1.call-done = bf16[768,2304]{1,0:T(8,128)(2,1)} async-done(((bf16[96,2304]{1,0:T(8,128)(2,1)}), bf16[768,2304]{1,0:T(8,128)(2,1)}) %all-gather.10.cloned.1.call-update) | async-done | bytes 3538960 | tf_op jit(solution)/shard_map/all_gather | solution.py:130
  83.3 4.2 fusion.129
  90.0 3.8 all-to-all-start.2
  93.9 32.9 %all_gather.58 = bf16[384,768]{0,1:T(8,128)(2,1)} all-gather(bf16[384,192]{0,1:T(8,128)(2,1)S(1)} %copy-done.26), channel_id=1, replica_groups=mesh['rows'=8,'head'=4] {'head'}, dimensions={1}, use_global_device_ids=true | all-gather | bytes 737280 | tf_op jit(solution)/shard_map/all_gather | solution.py:125
  126.8 5.1 all-gather.3
  131.9 18.8 %all-gather.4 = bf16[8,96,4]{1,2,0:T(4,128)(2,1)S(1)} all-gather(bf16[1,96,4]{1,2,0:T(4,128)(2,1)S(1)} %bitcast.452), channel_id=1, replica_groups=mesh['rows'=8,'head'=4] {'rows'}, dimensions={0}, use_global_device_ids=true | all-gather | bytes 6912 | tf_op jit(solution)/shard_map/all_gather | solution.py:135
  151.4 5.7 fusion.128
  157.1 4.3 copy.135
  161.4 4.5 all-to-all-start
  168.7 23.9 %while.45 = (s32[]{:T(128)}, bf16[4,512,3,64]{1,3,2,0:T(8,128)(2,1)}, f32[4,3,512]{2,1,0:T(4,128)S(1)}, bf16[4,512,3,64]{1,3,2,0:T(8,128)(2,1)S(1)}, s32[4]{0:T(...) while((s32[]{:T(128)}, ...), condition=%wide.region_11.12_spmd, body=%wide.region_8.11_spmd.sunk | while | flops 211385856 | bytes 11335809 | solution.py:188
  194.5 4.4 all-to-all-start.3
  198.9 2.7 slice_bitcast_fusion.3
  202.6 27.6 %while.44 = (s32[]{:T(128)}, bf16[4,512,3,64]{1,3,2,0:T(8,128)(2,1)}, f32[4,3,512]{2,1,0:T(4,128)S(1)}, bf16[4,512,3,64]{1,3,2,0:T(8,128)(2,1)}, s32[4]{0:T(128)...) while((s32[]{:T(128)}, ...), condition=%wide.region_3.4_spmd, body=%wide.region_0.3_spmd.sunk | while | flops 211385856 | bytes 11331713 | solution.py:188
  206.8 2.7 fusion.275
  213.7 2.7 fusion.275
  220.6 2.7 fusion.275
  227.5 2.7 fusion.275
  230.2 4.2 all-to-all-start.1
  234.5 2.7 fusion.199
  237.5 8.6 all-to-all-done.1
  246.1 3.8 fusion.198
  249.9 4.8 fusion.187
  257.4 31.4 %fusion.100 = (bf16[512,3072]{1,0:T(8,128)(2,1)}, bf16[512,3072]{1,0:T(8,128)(2,1)}, f32[512,3072]{1,0:T(8,128)}) fusion(f32[3072]{0:T(1024)S(1)} %add.262, f32[512,3072]{1,0:T(8,128)S(1)} %fusion.187, bf16[768,3072]{1,0:T(8,128)(2,1)S(1)} %copy-done.45, f32[512,768]{1,0:T(8,128)S(1)} %copy-done.20, f32[768]{0:T(1024)S(1)} %get-tuple-element.270, ...), kind=kOutput, calls=%fused_computation.133 | convolution fusion | flops 2625503232 | bytes 25188352 | tf_op jit(solution)/shard_map/dot_general | solution.py:197
  288.9 6.2 fusion.201
  295.5 2.8 fusion.200
  301.0 2.9 fusion.192
  303.9 8.4 fusion.202
  312.3 4.2 multiply_reduce_fusion.3
  316.6 5.0 fusion.203
  321.6 6.3 fusion.197
  333.7 3.0 convolution_convert_fusion.1
  339.0 3.5 all-to-all-start.4
  342.5 2.5 fusion.178
  345.1 3.3 convolution_add_fusion.4
  348.5 5.6 all-to-all-done.4
  354.1 3.5 all-to-all-start.6
  359.3 37.8 %while.46 = (s32[]{:T(128)}, bf16[4,512,3,3,64]{1,4,3,2,0:T(8,128)(2,1)}, bf16[4,512,3,64]{1,3,2,0:T(8,128)(2,1)S(1)}, s32[4]{0:T(128)S(1)}, s32[4]{0:T(128)S(1)...) while((s32[]{:T(128)}, ...), condition=%wide.region_22.23_spmd, body=%wide.region_20.22_spmd.sunk | while | flops 511999488 | bytes 27300500 | solution.py:224
  397.9 3.8 all-to-all-start.5
  403.5 42.0 %while.47 = (s32[]{:T(128)}, bf16[4,512,3,3,64]{1,4,3,2,0:T(8,128)(2,1)}, bf16[4,512,3,64]{1,3,2,0:T(8,128)(2,1)S(1)}, s32[4]{0:T(128)S(1)}, s32[4]{0:T(128)S(1)...) while((s32[]{:T(128)}, ...), condition=%wide.region_29.30_spmd, body=%wide.region_27.29_spmd.sunk | while | flops 511999488 | bytes 30446764 | solution.py:224
  446.9 3.6 all-to-all-start.7
  450.6 6.8 fusion.167
  457.4 21.6 %all-to-all-done.7 = bf16[4,512,1,576]{1,3,2,0:T(8,128)(2,1)S(1)} async-done(((bf16[4,512,1,576]{1,3,2,0:T(8,128)(2,1)}), bf16[4,512,1,576]{1,3,2,0:T(8,128)(2,1)S(1)}, u32[]{:S(2)}, u32[]{:S(2)}) %all-to-all-start.7) | async-done | bytes 2359328 | tf_op jit(solution)/shard_map/all_to_all | solution.py:114
  479.0 8.2 add_bitcast_fusion
  487.2 8.0 copy.160
  495.3 5.2 fusion.181
  500.6 5.6 convolution_add_fusion
  508.9 8.9 fusion.151
  517.9 11.8 convolution_add_fusion.1
  536.8 83.9 %reduce-scatter.31.cloned.1.call-done = f32[96,2304]{1,0:T(8,128)} async-done(((f32[768,2304]{1,0:T(8,128)}), f32[96,2304]{1,0:T(8,128)}) %reduce-scatter.31.cloned.1.call-update) | async-done | bytes 884752
  623.0 162.5 %reduce-scatter.29.cloned.1.call-done = f32[384,768]{1,0:T(8,128)} async-done(((f32[3072,768]{1,0:T(8,128)}), f32[384,768]{1,0:T(8,128)}) %reduce-scatter.29.cloned.1.call-update) | async-done | bytes 1179664 | tf_op jit(solution)/shard_map/reduce_scatter | solution.py:144
  793.9 56.8 %reduce-scatter.39.cloned.1.call-done = f32[96,4]{1,0:T(8,128)} async-done(((f32[768,4]{1,0:T(8,128)}), f32[96,4]{1,0:T(8,128)}) %reduce-scatter.39.cloned.1.call-update) | async-done | bytes 1552
  851.6 163.9 %reduce-scatter.25.cloned.1.call-done = f32[96,3072]{1,0:T(8,128)} async-done(((f32[768,3072]{1,0:T(8,128)}), f32[96,3072]{1,0:T(8,128)}) %reduce-scatter.25.cloned.1.call-update) | async-done | bytes 1179664 | tf_op jit(solution)/shard_map/reduce_scatter | solution.py:143
  1017.7 5.3 add_bitcast_fusion.2
  1027.0 53.0 %reduce-scatter.37.cloned.1.call-done = f32[96,8]{1,0:T(8,128)} async-done(((f32[768,8]{1,0:T(8,128)}), f32[96,8]{1,0:T(8,128)}) %reduce-scatter.37.cloned.1.call-update) | async-done | bytes 3088
  1080.9 5.7 all-reduce.2
  1088.2 13.6 %reduce-scatter.33.cloned.1.call-done = bf16[192,96]{1,0:T(8,128)(2,1)} async-done(((bf16[768,96]{1,0:T(8,128)(2,1)}), bf16[192,96]{1,0:T(8,128)(2,1)}) %reduce-scatter.33.cloned.1.call-update) | async-done | bytes 36880
  1103.4 22.9 %reduce-scatter.21.cloned.1.call-done = bf16[96,576]{0,1:T(8,128)(2,1)} async-done(((bf16[96,2304]{0,1:T(8,128)(2,1)}), bf16[96,576]{0,1:T(8,128)(2,1)}) %reduce-scatter.21.cloned.1.call-update) | async-done | bytes 110608 | tf_op jit(solution)/shard_map/reduce_scatter | solution.py:149
  1128.0 22.8 %reduce-scatter.35.cloned.1.call-done = bf16[192,384]{1,0:T(8,128)(2,1)} async-done(((bf16[768,384]{1,0:T(8,128)(2,1)}), bf16[192,384]{1,0:T(8,128)(2,1)}) %reduce-scatter.35.cloned.1.call-update) | async-done | bytes 147472
  1152.7 22.5 %reduce-scatter.27.cloned.1.call-done = bf16[96,768]{1,0:T(8,128)(2,1)} async-done(((bf16[96,3072]{1,0:T(8,128)(2,1)}), bf16[96,768]{1,0:T(8,128)(2,1)}) %reduce-scatter.27.cloned.1.call-update) | async-done | bytes 147472 | tf_op jit(solution)/shard_map/reduce_scatter | solution.py:155
  (417 shorter events, 188.9 us)
Async XLA Ops:
  7.2 17.8 %copy-start.25 = (bf16[96,768]{1,0:T(8,128)(2,1)S(1)}, bf16[96,768]{1,0:T(8,128)(2,1)}, u32[]{:S(2)}) copy-start(bf16[96,768]{1,0:T(8,128)(2,1)} %param.21) | copy-start | bytes 442372
  7.2 25.9 %copy-start.39 = (bf16[2,96]{1,0:T(2,128)(2,1)S(1)}, bf16[2,96]{1,0:T(2,128)(2,1)}, u32[]{:S(2)}) copy-start(bf16[2,96]{1,0:T(2,128)(2,1)} %param.23) | copy-start | bytes 1156
  7.2 76.1 %all-gather.10.cloned.1.call-start = ((), (), s32[]{:S(2)}) async-start(), calls=%async_computation.18 | async-start | bytes 3981312 | tf_op jit(solution)/shard_map/all_gather | solution.py:130
  17.5 216.9 %all-gather.12.cloned.1.call-start = ((), (), s32[]{:S(2)}) async-start(), calls=%async_computation.19 | async-start | bytes 1327104 | tf_op jit(solution)/shard_map/all_gather | solution.py:131
  24.9 225.0 %all-gather.14.cloned.1.call-start = ((), (), s32[]{:S(2)}) async-start(), calls=%async_computation.20 | async-start | bytes 5308416 | tf_op jit(solution)/shard_map/all_gather | solution.py:132
  90.0 36.8 %copy-start.40 = (bf16[1,96]{1,0:T(2,128)(2,1)S(1)}, bf16[1,96]{1,0:T(2,128)(2,1)}, u32[]{:S(2)}) copy-start(bf16[1,96]{1,0:T(2,128)(2,1)} %param.24) | copy-start | bytes 580
  90.0 61.3 %copy-start.37 = (s32[2,4]{1,0:T(2,128)S(1)}, s32[2,4]{1,0:T(2,128)}, u32[]{:S(2)}) copy-start(s32[2,4]{1,0:T(2,128)} %param.27) | copy-start | bytes 100
  90.0 61.3 %copy-start.38 = (s32[2,4]{1,0:T(2,128)S(1)}, s32[2,4]{1,0:T(2,128)}, u32[]{:S(2)}) copy-start(s32[2,4]{1,0:T(2,128)} %param.26) | copy-start | bytes 100
  90.0 71.3 %all-to-all-start.2 = ((bf16[1,512,4,576]{1,3,0,2:T(8,128)(2,1)}), bf16[1,512,4,576]{1,3,0,2:T(8,128)(2,1)S(1)}, u32[]{:S(2)}, u32[]{:S(2)}) async-start(bf16[1,512,4,576]{1,3,0,2:T(8,128)(2,1)} %bitcast.436), calls=%async_computation.2 | async-start | bytes 4718592 | tf_op jit(solution)/shard_map/all_to_all | solution.py:93
  93.8 195.0 %all-gather.16.cloned.1.call-start = ((), (), s32[]{:S(2)}) async-start(), calls=%async_computation.21 | async-start | bytes 5308416 | tf_op jit(solution)/shard_map/all_gather | solution.py:133
  151.4 144.1 %copy-start.27 = (f32[768]{0:T(1024)}, f32[768]{0:T(1024)S(1)}, u32[]{:S(2)}) copy-start(f32[768]{0:T(1024)S(1)} %get-tuple-element.270) | copy-start | bytes 9220
  161.4 4.6 copy-start.8
  161.4 33.1 %all-to-all-start = ((bf16[1,512,4,576]{1,3,0,2:T(8,128)(2,1)}), bf16[1,512,4,576]{1,3,0,2:T(8,128)(2,1)}, u32[]{:S(2)}, u32[]{:S(2)}) async-start(bf16[1,512,4,576]{1,3,0,2:T(8,128)(2,1)} %bitcast.52), calls=%async_computation | async-start | bytes 4718592 | tf_op jit(solution)/shard_map/all_to_all | solution.py:93
  192.7 6.2 copy-start.16
  192.7 6.2 copy-start.24
  192.7 6.2 copy-start.41
  192.7 6.2 copy-start.43
  192.7 9.0 copy-start.1
  192.7 9.0 copy-start.3
  194.5 35.7 %all-to-all-start.3 = ((bf16[4,512,1,192]{1,3,2,0:T(8,128)(2,1)}), bf16[4,512,1,192]{1,3,2,0:T(8,128)(2,1)}, u32[]{:S(2)}, u32[]{:S(2)}) async-start(bf16[4,512,1,192]{1,3,2,0:T(8,128)(2,1)} %bitcast.85), calls=%async_computation.3 | async-start | bytes 1572864 | tf_op jit(solution)/shard_map/all_to_all | solution.py:99
  230.2 4.2 copy-start.23
  230.2 15.9 %all-to-all-start.1 = ((bf16[4,512,1,192]{1,3,2,0:T(8,128)(2,1)}), bf16[4,512,1,192]{1,3,2,0:T(8,128)(2,1)}, u32[]{:S(2)}, u32[]{:S(2)}) async-start(bf16[4,512,1,192]{1,3,2,0:T(8,128)(2,1)} %bitcast.63), calls=%async_computation.1 | async-start | bytes 1572864 | tf_op jit(solution)/shard_map/all_to_all | solution.py:99
  237.2 90.8 %copy-start.5 = (f32[512,768]{1,0:T(8,128)}, f32[512,768]{1,0:T(8,128)S(1)}, u32[]{:S(2)}) copy-start(f32[512,768]{1,0:T(8,128)S(1)} %get-tuple-element.390) | copy-start | bytes 4718596
  249.9 4.9 copy-start.20
  249.9 7.5 copy-start.45
  257.4 31.5 %copy-start.36 = (f32[768]{0:T(1024)S(1)}, f32[768]{0:T(1024)}, u32[]{:S(2)}) copy-start(f32[768]{0:T(1024)} %get-tuple-element.264) | copy-start | bytes 9220
  288.9 6.6 copy-start.17
  288.9 6.6 copy-start.21
  288.9 6.6 copy-start.46
  300.9 11.4 slice-start
  300.9 15.6 %slice-start.2 = ((s8[6291456]{0:T(1024)(128)(4,1)}), s8[4194304]{0:T(1024)(128)(4,1)S(1)}, s32[]{:S(2)}) async-start(s8[6291456]{0:T(1024)(128)(4,1)} %bitcast.457), calls=%async_computation.34 | async-start | bytes 8388608
  303.9 8.5 copy-start.12
  303.9 17.7 %copy-start.10 = (f32[512,768]{1,0:T(8,128)}, f32[512,768]{1,0:T(8,128)S(1)}, u32[]{:S(2)}) copy-start(f32[512,768]{1,0:T(8,128)S(1)} %get-tuple-element.343) | copy-start | bytes 4718596
  303.9 8.5 slice-start.1
  303.9 12.7 %slice-start.3 = ((s8[6291456]{0:T(1024)(128)(4,1)}), s8[2097152]{0:T(1024)(128)(4,1)S(1)}, s32[]{:S(2)}) async-start(s8[6291456]{0:T(1024)(128)(4,1)} %bitcast.457), calls=%async_computation.35 | async-start | bytes 4194304
  321.6 6.4 copy-start.18
  328.5 5.2 copy-start.22
  339.0 15.1 %all-to-all-start.4 = ((bf16[1,512,4,192]{1,3,0,2:T(8,128)(2,1)}), bf16[1,512,4,192]{1,3,0,2:T(8,128)(2,1)S(1)}, u32[]{:S(2)}, u32[]{:S(2)}) async-start(bf16[1,512,4,192]{1,3,0,2:T(8,128)(2,1)} %bitcast.92), calls=%async_computation.4 | async-start | bytes 1572864 | tf_op jit(solution)/shard_map/all_to_all | solution.py:108
  342.5 192.4 %reduce-scatter.23.cloned.1.call-start = ((), (), s32[]{:S(2)}) async-start(), calls=%async_computation.23 | async-start | bytes 2654208 | tf_op jit(solution)/shard_map/reduce_scatter | solution.py:142
  354.1 43.0 %all-to-all-start.6 = ((bf16[1,512,4,192]{1,3,0,2:T(8,128)(2,1)}), bf16[1,512,4,192]{1,3,0,2:T(8,128)(2,1)S(1)}, u32[]{:S(2)}, u32[]{:S(2)}) async-start(bf16[1,512,4,192]{1,3,0,2:T(8,128)(2,1)} %bitcast.437), calls=%async_computation.6 | async-start | bytes 1572864 | tf_op jit(solution)/shard_map/all_to_all | solution.py:108
  397.0 6.5 copy-start.2
  397.0 6.5 copy-start.42
  397.0 6.5 copy-start.44
  397.9 47.6 %all-to-all-start.5 = ((bf16[4,512,1,576]{1,3,2,0:T(8,128)(2,1)}), bf16[4,512,1,576]{1,3,2,0:T(8,128)(2,1)S(1)}, u32[]{:S(2)}, u32[]{:S(2)}) async-start(bf16[4,512,1,576]{1,3,2,0:T(8,128)(2,1)} %bitcast.97), calls=%async_computation.5 | async-start | bytes 4718592 | tf_op jit(solution)/shard_map/all_to_all | solution.py:114
  403.5 5.1 copy-start.4
  414.0 5.1 copy-start.4
  424.4 5.1 copy-start.4
  435.0 5.1 copy-start.4
  446.9 32.1 %all-to-all-start.7 = ((bf16[4,512,1,576]{1,3,2,0:T(8,128)(2,1)}), bf16[4,512,1,576]{1,3,2,0:T(8,128)(2,1)S(1)}, u32[]{:S(2)}, u32[]{:S(2)}) async-start(bf16[4,512,1,576]{1,3,2,0:T(8,128)(2,1)} %bitcast.109), calls=%async_computation.7 | async-start | bytes 4718592 | tf_op jit(solution)/shard_map/all_to_all | solution.py:114
  450.6 170.1 %reduce-scatter.31.cloned.1.call-start = ((), (), s32[]{:S(2)}) async-start(), calls=%async_computation.27 | async-start | bytes 7962624
  495.2 290.3 %reduce-scatter.29.cloned.1.call-start = ((), (), s32[]{:S(2)}) async-start(), calls=%async_computation.26 | async-start | bytes 10616832 | tf_op jit(solution)/shard_map/reduce_scatter | solution.py:144
  495.3 5.3 copy-start.9
  495.3 5.3 copy-start.11
  506.2 344.5 %reduce-scatter.39.cloned.1.call-start = ((), (), s32[]{:S(2)}) async-start(), calls=%async_computation.31 | async-start | bytes 442368
  517.9 497.6 %reduce-scatter.25.cloned.1.call-start = ((), (), s32[]{:S(2)}) async-start(), calls=%async_computation.24 | async-start | bytes 10616832 | tf_op jit(solution)/shard_map/reduce_scatter | solution.py:143
  529.7 550.3 %reduce-scatter.37.cloned.1.call-start = ((), (), s32[]{:S(2)}) async-start(), calls=%async_computation.30 | async-start | bytes 442368
  534.8 567.1 %reduce-scatter.33.cloned.1.call-start = ((), (), s32[]{:S(2)}) async-start(), calls=%async_computation.28 | async-start | bytes 245760
  535.9 254.3 %copy-start.49 = (u32[32]{0:T(128)S(1)}, u32[32]{0:T(128)}, u32[]{:S(2)}) copy-start(u32[32]{0:T(128)} %constant.177) | copy-start | bytes 388
  535.9 255.6 %copy-start.19 = (bf16[1,1,512,768]{3,2,1,0:T(8,128)(2,1)S(1)}, bf16[1,1,512,768]{3,2,1,0:T(8,128)(2,1)}, u32[]{:S(2)}) copy-start(bf16[1,1,512,768]{3,2,1,0:T(8,128)(2,1)} %get-tuple-element.373) | copy-start | bytes 2359300
  536.7 589.6 %reduce-scatter.21.cloned.1.call-start = ((), (), s32[]{:S(2)}) async-start(), calls=%async_computation.22 | async-start | bytes 737280 | tf_op jit(solution)/shard_map/reduce_scatter | solution.py:149
  623.0 527.9 %reduce-scatter.35.cloned.1.call-start = ((), (), s32[]{:S(2)}) async-start(), calls=%async_computation.29 | async-start | bytes 737280
  789.9 385.4 %reduce-scatter.27.cloned.1.call-start = ((), (), s32[]{:S(2)}) async-start(), calls=%async_computation.25 | async-start | bytes 737280 | tf_op jit(solution)/shard_map/reduce_scatter | solution.py:155
  1017.7 5.4 copy-start.15
  1017.7 5.4 copy-start.47
  (17 other events, 35.8 us)
Sparse Core Ops, SparseCore 0:
  17.6 65.6 all-gather.9
  86.1 39.7 all-gather.11
  128.1 78.0 all-gather.13
  208.1 78.9 all-gather.15
  348.6 67.5 reduce-scatter.22
  495.3 125.2 reduce-scatter.30
  624.3 161.2 reduce-scatter.28
  789.4 61.2 reduce-scatter.38
  854.3 161.1 reduce-scatter.24
  1018.6 61.3 reduce-scatter.36
  1083.0 18.7 reduce-scatter.32
  1104.2 22.0 reduce-scatter.20
  1128.8 22.0 reduce-scatter.34
  1153.2 22.0 reduce-scatter.26
where the time goes:
time: 1190 us; the launch traced here: 1180 us
  waiting for transfers between devices  657 us (55%)
  matrix products  213 us (18%)
  blocking collectives  117 us (10%)
  local copies, waits for them, and re-layouts  79.6 us (7%)
  other arithmetic  68.8 us (6%)
  starting transfers between devices  32.3 us (3%)
  between operations  16 us (1%)
    unnamed x19, waiting for transfers between devices  230 us
    reduce_scatter x1, waiting for transfers between devices, reduce_grads(): lax.psum_scatter(running[2], 'rows', scatter_dimension=0, tiled=True)  164 us
    reduce_scatter x1, waiting for transfers between devices, reduce_grads(): lax.psum_scatter(running[3], 'rows', scatter_dimension=0, tiled=True)  163 us
    dot_general x8, matrix products, contract_rows(): lax.dot_general(left, right, (((0,), (0,)), ((), ())), preferred_element_...  52.4 us
    dot_general x2, matrix products, layer_step(): jnp.dot(hidden_low, up_full, preferred_element_type=jnp.float32)  36.3 us
    dot_general x8, matrix products, contract_cols(): lax.dot_general(left, right, (((1,), (1,)), ((), ())), preferred_element_...  36.1 us
    all_gather x1, blocking collectives, gather_weights(): lax.all_gather(down_weight, 'head', axis=1, tiled=True)  32.9 us
    unnamed x126, local copies, waits for them, and re-layouts  30.5 us
  transfers between devices with their start and end apart: 22, of which 14 were waited for; matrix products, arithmetic and copies ran while one was open for 26% of the time, Pallas kernels for 0%

commit v1 on v0

--- a/solution.py
+++ b/solution.py
@@ -111,8 +111,16 @@
 
 def grad_to_tokens(grad_items, seq_per):
     width = grad_items.shape[2] * 3 * HD
-    joined = lax.all_to_all(
-        grad_items.reshape(-1, SEQ, 1, width), "head", split_axis=0, concat_axis=2, tiled=True
+    joined = jnp.concatenate(
+        lax.all_to_all(
+            jnp.stack(
+                jnp.split(grad_items.reshape(-1, SEQ, 1, width), lax.axis_size("head"), axis=0)
+            ),
+            "head",
+            0,
+            0,
+        ),
+        axis=2,
     )
     return joined.reshape(seq_per * SEQ, 3 * D)
 

time: 1190 us -> 1200 us (level)
    unnamed x126 -> x128, local copies, waits for them, and re-layouts: 30.5 us -> 30.6 us
where the time goes in v1:
time: 1200 us; the launch traced here: 1190 us
  waiting for transfers between devices  657 us (55%)
  matrix products  213 us (18%)
  blocking collectives  117 us (10%)
  local copies, waits for them, and re-layouts  83.1 us (7%)
  other arithmetic  72.2 us (6%)
  starting transfers between devices  32.3 us (3%)
  between operations  16 us (1%)
    unnamed x19, waiting for transfers between devices  230 us
    reduce_scatter x1, waiting for transfers between devices, reduce_grads(): lax.psum_scatter(running[2], 'rows', scatter_dimension=0, tiled=True)  164 us
    reduce_scatter x1, waiting for transfers between devices, reduce_grads(): lax.psum_scatter(running[3], 'rows', scatter_dimension=0, tiled=True)  163 us
    dot_general x8, matrix products, contract_rows(): lax.dot_general(left, right, (((0,), (0,)), ((), ())), preferred_element_...  52.4 us
    dot_general x8, matrix products, contract_cols(): lax.dot_general(left, right, (((1,), (1,)), ((), ())), preferred_element_...  36.7 us
    dot_general x2, matrix products, layer_step(): jnp.dot(hidden_low, up_full, preferred_element_type=jnp.float32)  36.3 us
    all_gather x1, blocking collectives, gather_weights(): lax.all_gather(down_weight, 'head', axis=1, tiled=True)  32.9 us
    unnamed x128, local copies, waits for them, and re-layouts  30.6 us
  transfers between devices with their start and end apart: 22, of which 14 were waited for; matrix products, arithmetic and copies ran while one was open for 26% of the time, Pallas kernels for 0%

profile of v1, /device:TPU:0, one launch (start us, length us, event | category | flops | bytes accessed | tf_op | source)
XLA Modules:
  0.0 1191.1 jit_solution(2883270533605068719)
XLA Ops:
  7.2 8.8 all-gather
  18.5 5.6 all_gather.52
  25.0 8.1 all_gather.56
  33.1 5.1 all-gather.1
  38.1 27.4 %all-gather.2 = bf16[8,96,8]{1,2,0:T(8,128)(2,1)S(1)} all-gather(bf16[1,96,8]{1,2,0:T(8,128)(2,1)S(1)} %bitcast.457), channel_id=1, replica_groups=mesh['rows'=8,'head'=4] {'rows'}, dimensions={0}, use_global_device_ids=true | all-gather | bytes 13824 | tf_op jit(solution)/shard_map/all_gather | solution.py:142
  66.6 16.7 %all-gather.10.cloned.1.call-done = bf16[768,2304]{1,0:T(8,128)(2,1)} async-done(((bf16[96,2304]{1,0:T(8,128)(2,1)}), bf16[768,2304]{1,0:T(8,128)(2,1)}) %all-gather.10.cloned.1.call-update) | async-done | bytes 3538960 | tf_op jit(solution)/shard_map/all_gather | solution.py:138
  83.3 4.2 fusion.129
  90.0 3.8 all-to-all-start.2
  93.9 32.9 %all_gather.58 = bf16[384,768]{0,1:T(8,128)(2,1)} all-gather(bf16[384,192]{0,1:T(8,128)(2,1)S(1)} %copy-done.26), channel_id=1, replica_groups=mesh['rows'=8,'head'=4] {'head'}, dimensions={1}, use_global_device_ids=true | all-gather | bytes 737280 | tf_op jit(solution)/shard_map/all_gather | solution.py:133
  126.8 5.1 all-gather.3
  131.9 18.8 %all-gather.4 = bf16[8,96,4]{1,2,0:T(4,128)(2,1)S(1)} all-gather(bf16[1,96,4]{1,2,0:T(4,128)(2,1)S(1)} %bitcast.458), channel_id=1, replica_groups=mesh['rows'=8,'head'=4] {'rows'}, dimensions={0}, use_global_device_ids=true | all-gather | bytes 6912 | tf_op jit(solution)/shard_map/all_gather | solution.py:143
  151.4 5.7 fusion.128
  157.1 4.3 copy.155
  161.4 4.5 all-to-all-start
  168.7 23.9 %while.45 = (s32[]{:T(128)}, bf16[4,512,3,64]{1,3,2,0:T(8,128)(2,1)}, f32[4,3,512]{2,1,0:T(4,128)S(1)}, bf16[4,512,3,64]{1,3,2,0:T(8,128)(2,1)S(1)}, s32[4]{0:T(...) while((s32[]{:T(128)}, ...), condition=%wide.region_11.12_spmd, body=%wide.region_8.11_spmd.sunk | while | flops 211385856 | bytes 11335809 | solution.py:196
  194.5 4.4 all-to-all-start.3
  198.9 2.7 slice_bitcast_fusion.3
  202.6 27.6 %while.44 = (s32[]{:T(128)}, bf16[4,512,3,64]{1,3,2,0:T(8,128)(2,1)}, f32[4,3,512]{2,1,0:T(4,128)S(1)}, bf16[4,512,3,64]{1,3,2,0:T(8,128)(2,1)}, s32[4]{0:T(128)...) while((s32[]{:T(128)}, ...), condition=%wide.region_3.4_spmd, body=%wide.region_0.3_spmd.sunk | while | flops 211385856 | bytes 11331713 | solution.py:196
  206.8 2.7 fusion.277
  213.7 2.7 fusion.277
  220.6 2.7 fusion.277
  227.5 2.7 fusion.277
  230.2 4.2 all-to-all-start.1
  234.5 2.7 fusion.201
  237.5 8.6 all-to-all-done.1
  246.1 3.8 fusion.200
  249.9 4.9 fusion.187
  257.4 31.4 %fusion.100 = (bf16[512,3072]{1,0:T(8,128)(2,1)}, bf16[512,3072]{1,0:T(8,128)(2,1)}, f32[512,3072]{1,0:T(8,128)}) fusion(f32[3072]{0:T(1024)S(1)} %add.262, f32[512,3072]{1,0:T(8,128)S(1)} %fusion.187, bf16[768,3072]{1,0:T(8,128)(2,1)S(1)} %copy-done.46, f32[512,768]{1,0:T(8,128)S(1)} %copy-done.20, f32[768]{0:T(1024)S(1)} %get-tuple-element.270, ...), kind=kOutput, calls=%fused_computation.133 | convolution fusion | flops 2625503232 | bytes 25188352 | tf_op jit(solution)/shard_map/dot_general | solution.py:205
  288.9 6.2 fusion.203
  295.6 2.8 fusion.202
  301.0 2.9 fusion.192
  303.9 8.4 fusion.204
  312.4 4.2 multiply_reduce_fusion.3
  316.6 5.6 fusion.205
  322.2 6.3 fusion.197
  334.3 3.0 convolution_convert_fusion.1
  339.6 3.5 all-to-all-start.4
  343.1 2.5 fusion.178
  345.7 3.3 convolution_add_fusion.4
  349.1 5.6 all-to-all-done.4
  354.7 3.5 all-to-all-start.6
  359.8 37.8 %while.46 = (s32[]{:T(128)}, bf16[4,512,3,3,64]{1,4,3,2,0:T(8,128)(2,1)}, bf16[4,512,3,64]{1,3,2,0:T(8,128)(2,1)S(1)}, s32[4]{0:T(128)S(1)}, s32[4]{0:T(128)S(1)...) while((s32[]{:T(128)}, ...), condition=%wide.region_22.23_spmd, body=%wide.region_20.22_spmd.sunk | while | flops 511999488 | bytes 27300500 | solution.py:232
  402.0 3.8 all-to-all-start.5
  407.5 41.8 %while.47 = (s32[]{:T(128)}, bf16[4,512,3,3,64]{1,4,3,2,0:T(8,128)(2,1)}, bf16[4,512,3,64]{1,3,2,0:T(8,128)(2,1)S(1)}, s32[4]{0:T(128)S(1)}, s32[4]{0:T(128)S(1)...) while((s32[]{:T(128)}, ...), condition=%wide.region_29.30_spmd, body=%wide.region_27.29_spmd.sunk | while | flops 511999488 | bytes 30446764 | solution.py:232
  454.3 3.6 all-to-all-start.7
  458.0 6.8 fusion.167
  464.7 21.6 %all-to-all-done.7 = bf16[4,1,512,1,576]{2,4,3,1,0:T(8,128)(2,1)S(1)} async-done(((bf16[4,1,512,1,576]{2,4,3,1,0:T(8,128)(2,1)}), bf16[4,1,512,1,576]{2,4,3,1,0:T(8,128)(2,1)S(1)}, u32[]{:S(2)}, u32[]{:S(2)}) %all-to-all-start.7) | async-done | bytes 2359328 | tf_op jit(solution)/shard_map/all_to_all | solution.py:115
  486.3 8.2 add_bitcast_fusion
  494.5 8.0 copy.184
  502.6 5.2 fusion.181
  507.9 5.6 convolution_add_fusion
  516.3 8.9 fusion.151
  525.3 11.8 convolution_add_fusion.1
  544.2 83.8 %reduce-scatter.31.cloned.1.call-done = f32[96,2304]{1,0:T(8,128)} async-done(((f32[768,2304]{1,0:T(8,128)}), f32[96,2304]{1,0:T(8,128)}) %reduce-scatter.31.cloned.1.call-update) | async-done | bytes 884752
  630.3 162.5 %reduce-scatter.29.cloned.1.call-done = f32[384,768]{1,0:T(8,128)} async-done(((f32[3072,768]{1,0:T(8,128)}), f32[384,768]{1,0:T(8,128)}) %reduce-scatter.29.cloned.1.call-update) | async-done | bytes 1179664 | tf_op jit(solution)/shard_map/reduce_scatter | solution.py:152
  801.2 56.8 %reduce-scatter.39.cloned.1.call-done = f32[96,4]{1,0:T(8,128)} async-done(((f32[768,4]{1,0:T(8,128)}), f32[96,4]{1,0:T(8,128)}) %reduce-scatter.39.cloned.1.call-update) | async-done | bytes 1552
  858.9 163.9 %reduce-scatter.25.cloned.1.call-done = f32[96,3072]{1,0:T(8,128)} async-done(((f32[768,3072]{1,0:T(8,128)}), f32[96,3072]{1,0:T(8,128)}) %reduce-scatter.25.cloned.1.call-update) | async-done | bytes 1179664 | tf_op jit(solution)/shard_map/reduce_scatter | solution.py:151
  1025.0 5.3 add_bitcast_fusion.2
  1034.3 52.9 %reduce-scatter.37.cloned.1.call-done = f32[96,8]{1,0:T(8,128)} async-done(((f32[768,8]{1,0:T(8,128)}), f32[96,8]{1,0:T(8,128)}) %reduce-scatter.37.cloned.1.call-update) | async-done | bytes 3088
  1088.1 5.7 all-reduce.2
  1095.4 13.6 %reduce-scatter.33.cloned.1.call-done = bf16[192,96]{1,0:T(8,128)(2,1)} async-done(((bf16[768,96]{1,0:T(8,128)(2,1)}), bf16[192,96]{1,0:T(8,128)(2,1)}) %reduce-scatter.33.cloned.1.call-update) | async-done | bytes 36880
  1110.6 22.9 %reduce-scatter.21.cloned.1.call-done = bf16[96,576]{0,1:T(8,128)(2,1)} async-done(((bf16[96,2304]{0,1:T(8,128)(2,1)}), bf16[96,576]{0,1:T(8,128)(2,1)}) %reduce-scatter.21.cloned.1.call-update) | async-done | bytes 110608 | tf_op jit(solution)/shard_map/reduce_scatter | solution.py:157
  1135.2 22.8 %reduce-scatter.35.cloned.1.call-done = bf16[192,384]{1,0:T(8,128)(2,1)} async-done(((bf16[768,384]{1,0:T(8,128)(2,1)}), bf16[192,384]{1,0:T(8,128)(2,1)}) %reduce-scatter.35.cloned.1.call-update) | async-done | bytes 147472
  1159.9 22.5 %reduce-scatter.27.cloned.1.call-done = bf16[96,768]{1,0:T(8,128)(2,1)} async-done(((bf16[96,3072]{1,0:T(8,128)(2,1)}), bf16[96,768]{1,0:T(8,128)(2,1)}) %reduce-scatter.27.cloned.1.call-update) | async-done | bytes 147472 | tf_op jit(solution)/shard_map/reduce_scatter | solution.py:163
  (423 shorter events, 195.6 us)
Async XLA Ops:
  7.2 17.8 %copy-start.25 = (bf16[96,768]{1,0:T(8,128)(2,1)S(1)}, bf16[96,768]{1,0:T(8,128)(2,1)}, u32[]{:S(2)}) copy-start(bf16[96,768]{1,0:T(8,128)(2,1)} %param.21) | copy-start | bytes 442372
  7.2 25.9 %copy-start.40 = (bf16[2,96]{1,0:T(2,128)(2,1)S(1)}, bf16[2,96]{1,0:T(2,128)(2,1)}, u32[]{:S(2)}) copy-start(bf16[2,96]{1,0:T(2,128)(2,1)} %param.23) | copy-start | bytes 1156
  7.2 76.1 %all-gather.10.cloned.1.call-start = ((), (), s32[]{:S(2)}) async-start(), calls=%async_computation.18 | async-start | bytes 3981312 | tf_op jit(solution)/shard_map/all_gather | solution.py:138
  17.5 216.9 %all-gather.12.cloned.1.call-start = ((), (), s32[]{:S(2)}) async-start(), calls=%async_computation.19 | async-start | bytes 1327104 | tf_op jit(solution)/shard_map/all_gather | solution.py:139
  24.9 225.0 %all-gather.14.cloned.1.call-start = ((), (), s32[]{:S(2)}) async-start(), calls=%async_computation.20 | async-start | bytes 5308416 | tf_op jit(solution)/shard_map/all_gather | solution.py:140
  90.0 36.8 %copy-start.41 = (bf16[1,96]{1,0:T(2,128)(2,1)S(1)}, bf16[1,96]{1,0:T(2,128)(2,1)}, u32[]{:S(2)}) copy-start(bf16[1,96]{1,0:T(2,128)(2,1)} %param.24) | copy-start | bytes 580
  90.0 61.3 %copy-start.38 = (s32[2,4]{1,0:T(2,128)S(1)}, s32[2,4]{1,0:T(2,128)}, u32[]{:S(2)}) copy-start(s32[2,4]{1,0:T(2,128)} %param.27) | copy-start | bytes 100
  90.0 61.3 %copy-start.39 = (s32[2,4]{1,0:T(2,128)S(1)}, s32[2,4]{1,0:T(2,128)}, u32[]{:S(2)}) copy-start(s32[2,4]{1,0:T(2,128)} %param.26) | copy-start | bytes 100
  90.0 71.3 %all-to-all-start.2 = ((bf16[1,512,4,576]{1,3,0,2:T(8,128)(2,1)}), bf16[1,512,4,576]{1,3,0,2:T(8,128)(2,1)S(1)}, u32[]{:S(2)}, u32[]{:S(2)}) async-start(bf16[1,512,4,576]{1,3,0,2:T(8,128)(2,1)} %bitcast.434), calls=%async_computation.2 | async-start | bytes 4718592 | tf_op jit(solution)/shard_map/all_to_all | solution.py:93
  93.8 195.1 %all-gather.16.cloned.1.call-start = ((), (), s32[]{:S(2)}) async-start(), calls=%async_computation.21 | async-start | bytes 5308416 | tf_op jit(solution)/shard_map/all_gather | solution.py:141
  151.4 144.1 %copy-start.27 = (f32[768]{0:T(1024)}, f32[768]{0:T(1024)S(1)}, u32[]{:S(2)}) copy-start(f32[768]{0:T(1024)S(1)} %get-tuple-element.270) | copy-start | bytes 9220
  161.4 4.6 copy-start.8
  161.4 33.1 %all-to-all-start = ((bf16[1,512,4,576]{1,3,0,2:T(8,128)(2,1)}), bf16[1,512,4,576]{1,3,0,2:T(8,128)(2,1)}, u32[]{:S(2)}, u32[]{:S(2)}) async-start(bf16[1,512,4,576]{1,3,0,2:T(8,128)(2,1)} %bitcast.52), calls=%async_computation | async-start | bytes 4718592 | tf_op jit(solution)/shard_map/all_to_all | solution.py:93
  192.7 6.2 copy-start.16
  192.7 6.2 copy-start.24
  192.7 6.2 copy-start.42
  192.7 6.2 copy-start.44
  192.7 9.0 copy-start.1
  192.7 9.0 copy-start.3
  194.5 35.7 %all-to-all-start.3 = ((bf16[4,512,1,192]{1,3,2,0:T(8,128)(2,1)}), bf16[4,512,1,192]{1,3,2,0:T(8,128)(2,1)}, u32[]{:S(2)}, u32[]{:S(2)}) async-start(bf16[4,512,1,192]{1,3,2,0:T(8,128)(2,1)} %bitcast.85), calls=%async_computation.3 | async-start | bytes 1572864 | tf_op jit(solution)/shard_map/all_to_all | solution.py:99
  230.2 4.2 copy-start.23
  230.2 15.9 %all-to-all-start.1 = ((bf16[4,512,1,192]{1,3,2,0:T(8,128)(2,1)}), bf16[4,512,1,192]{1,3,2,0:T(8,128)(2,1)}, u32[]{:S(2)}, u32[]{:S(2)}) async-start(bf16[4,512,1,192]{1,3,2,0:T(8,128)(2,1)} %bitcast.63), calls=%async_computation.1 | async-start | bytes 1572864 | tf_op jit(solution)/shard_map/all_to_all | solution.py:99
  237.2 91.4 %copy-start.5 = (f32[512,768]{1,0:T(8,128)}, f32[512,768]{1,0:T(8,128)S(1)}, u32[]{:S(2)}) copy-start(f32[512,768]{1,0:T(8,128)S(1)} %get-tuple-element.398) | copy-start | bytes 4718596
  249.9 4.9 copy-start.20
  249.9 7.5 copy-start.46
  257.4 31.5 %copy-start.37 = (f32[768]{0:T(1024)S(1)}, f32[768]{0:T(1024)}, u32[]{:S(2)}) copy-start(f32[768]{0:T(1024)} %get-tuple-element.264) | copy-start | bytes 9220
  288.9 6.6 copy-start.17
  288.9 6.6 copy-start.21
  288.9 6.6 copy-start.47
  301.0 11.4 slice-start
  301.0 15.6 %slice-start.2 = ((s8[6291456]{0:T(1024)(128)(4,1)}), s8[4194304]{0:T(1024)(128)(4,1)S(1)}, s32[]{:S(2)}) async-start(s8[6291456]{0:T(1024)(128)(4,1)} %bitcast.463), calls=%async_computation.34 | async-start | bytes 8388608
  303.9 8.5 copy-start.12
  303.9 18.3 %copy-start.10 = (f32[512,768]{1,0:T(8,128)}, f32[512,768]{1,0:T(8,128)S(1)}, u32[]{:S(2)}) copy-start(f32[512,768]{1,0:T(8,128)S(1)} %get-tuple-element.343) | copy-start | bytes 4718596
  303.9 8.5 slice-start.1
  303.9 12.7 %slice-start.3 = ((s8[6291456]{0:T(1024)(128)(4,1)}), s8[2097152]{0:T(1024)(128)(4,1)S(1)}, s32[]{:S(2)}) async-start(s8[6291456]{0:T(1024)(128)(4,1)} %bitcast.463), calls=%async_computation.35 | async-start | bytes 4194304
  322.2 6.3 copy-start.18
  329.1 5.2 copy-start.22
  339.6 15.1 %all-to-all-start.4 = ((bf16[1,512,4,192]{1,3,0,2:T(8,128)(2,1)}), bf16[1,512,4,192]{1,3,0,2:T(8,128)(2,1)S(1)}, u32[]{:S(2)}, u32[]{:S(2)}) async-start(bf16[1,512,4,192]{1,3,0,2:T(8,128)(2,1)} %bitcast.92), calls=%async_computation.4 | async-start | bytes 1572864 | tf_op jit(solution)/shard_map/all_to_all | solution.py:108
  343.1 199.2 %reduce-scatter.23.cloned.1.call-start = ((), (), s32[]{:S(2)}) async-start(), calls=%async_computation.23 | async-start | bytes 2654208 | tf_op jit(solution)/shard_map/reduce_scatter | solution.py:150
  354.7 46.4 %all-to-all-start.6 = ((bf16[1,512,4,192]{1,3,0,2:T(8,128)(2,1)}), bf16[1,512,4,192]{1,3,0,2:T(8,128)(2,1)S(1)}, u32[]{:S(2)}, u32[]{:S(2)}) async-start(bf16[1,512,4,192]{1,3,0,2:T(8,128)(2,1)} %bitcast.435), calls=%async_computation.6 | async-start | bytes 1572864 | tf_op jit(solution)/shard_map/all_to_all | solution.py:108
  401.1 6.4 copy-start.2
  401.1 6.4 copy-start.43
  401.1 6.4 copy-start.45
  402.0 50.9 %all-to-all-start.5 = ((bf16[4,1,512,1,576]{2,4,3,1,0:T(8,128)(2,1)}), bf16[4,1,512,1,576]{2,4,3,1,0:T(8,128)(2,1)S(1)}, u32[]{:S(2)}, u32[]{:S(2)}) async-start(bf16[4,1,512,1,576]{2,4,3,1,0:T(8,128)(2,1)} %pad_maximum_fusion.3), calls=%async_computation.5 | async-start | bytes 4718592 | tf_op jit(solution)/shard_map/all_to_all | solution.py:115
  407.5 5.1 copy-start.4
  418.0 5.1 copy-start.4
  428.4 5.1 copy-start.4
  438.9 5.1 copy-start.4
  454.3 32.1 %all-to-all-start.7 = ((bf16[4,1,512,1,576]{2,4,3,1,0:T(8,128)(2,1)}), bf16[4,1,512,1,576]{2,4,3,1,0:T(8,128)(2,1)S(1)}, u32[]{:S(2)}, u32[]{:S(2)}) async-start(bf16[4,1,512,1,576]{2,4,3,1,0:T(8,128)(2,1)} %pad_maximum_fusion.4), calls=%async_computation.7 | async-start | bytes 4718592 | tf_op jit(solution)/shard_map/all_to_all | solution.py:115
  457.9 170.1 %reduce-scatter.31.cloned.1.call-start = ((), (), s32[]{:S(2)}) async-start(), calls=%async_computation.27 | async-start | bytes 7962624
  502.6 290.3 %reduce-scatter.29.cloned.1.call-start = ((), (), s32[]{:S(2)}) async-start(), calls=%async_computation.26 | async-start | bytes 10616832 | tf_op jit(solution)/shard_map/reduce_scatter | solution.py:152
  502.6 5.3 copy-start.9
  502.6 5.3 copy-start.11
  513.5 344.5 %reduce-scatter.39.cloned.1.call-start = ((), (), s32[]{:S(2)}) async-start(), calls=%async_computation.31 | async-start | bytes 442368
  525.2 497.6 %reduce-scatter.25.cloned.1.call-start = ((), (), s32[]{:S(2)}) async-start(), calls=%async_computation.24 | async-start | bytes 10616832 | tf_op jit(solution)/shard_map/reduce_scatter | solution.py:151
  537.1 550.1 %reduce-scatter.37.cloned.1.call-start = ((), (), s32[]{:S(2)}) async-start(), calls=%async_computation.30 | async-start | bytes 442368
  542.2 566.9 %reduce-scatter.33.cloned.1.call-start = ((), (), s32[]{:S(2)}) async-start(), calls=%async_computation.28 | async-start | bytes 245760
  543.2 254.3 %copy-start.50 = (u32[32]{0:T(128)S(1)}, u32[32]{0:T(128)}, u32[]{:S(2)}) copy-start(u32[32]{0:T(128)} %constant.177) | copy-start | bytes 388
  543.3 255.5 %copy-start.19 = (bf16[1,1,512,768]{3,2,1,0:T(8,128)(2,1)S(1)}, bf16[1,1,512,768]{3,2,1,0:T(8,128)(2,1)}, u32[]{:S(2)}) copy-start(bf16[1,1,512,768]{3,2,1,0:T(8,128)(2,1)} %get-tuple-element.381) | copy-start | bytes 2359300
  544.1 589.3 %reduce-scatter.21.cloned.1.call-start = ((), (), s32[]{:S(2)}) async-start(), calls=%async_computation.22 | async-start | bytes 737280 | tf_op jit(solution)/shard_map/reduce_scatter | solution.py:157
  630.3 527.8 %reduce-scatter.35.cloned.1.call-start = ((), (), s32[]{:S(2)}) async-start(), calls=%async_computation.29 | async-start | bytes 737280
  797.2 385.3 %reduce-scatter.27.cloned.1.call-start = ((), (), s32[]{:S(2)}) async-start(), calls=%async_computation.25 | async-start | bytes 737280 | tf_op jit(solution)/shard_map/reduce_scatter | solution.py:163
  1025.0 5.4 copy-start.15
  1025.0 5.4 copy-start.48
  (18 other events, 36.6 us)
Sparse Core Ops, SparseCore 0:
  17.6 65.6 all-gather.9
  86.1 39.7 all-gather.11
  128.1 78.0 all-gather.13
  208.1 78.9 all-gather.15
  349.2 67.3 reduce-scatter.22
  502.7 125.2 reduce-scatter.30
  631.6 161.2 reduce-scatter.28
  796.7 61.2 reduce-scatter.38
  861.6 161.1 reduce-scatter.24
  1025.9 61.2 reduce-scatter.36
  1090.2 18.7 reduce-scatter.32
  1111.4 22.0 reduce-scatter.20
  1136.0 22.0 reduce-scatter.34
  1160.4 22.0 reduce-scatter.26
